TPU v7x, 32 devices: a whole 2x2x4 slice. The times are simulated.
32 devices in a mesh: pipe: 4 (over x, core), expert: 4 (over z), tensor: 2 (over y).
Axes of the slice: x: 2, y: 2, z: 4, core: 2. Of those that a mesh axis runs over, the one named last changes fastest.
Arguments:
- stream: bfloat16 [2, 4, 64, 7168], P(None, 'pipe', 'expert', 'tensor'), may hold values from -6 to 6
- expert_ids: int32 [2, 4, 64, 2], P(None, 'pipe', 'expert'), may hold values from 0 to 3, all different within a row; in each aligned block of 16 rows (0 to 15, 16 to 31, ..., all dimensions but the last counted through in order) at most 12 rows name the same one
- norm_gain: float32 [4, 7168], P('pipe', 'tensor'), may hold values from 0.1 to 1.9
- router: float32 [4, 7168, 4], P('pipe', 'tensor'), may hold values from -0.0625 to 0.0625
- w_up: bfloat16 [4, 7168, 1024], P('expert', 'tensor'), may hold values from -0.0625 to 0.0625
- w_down: bfloat16 [4, 1024, 7168], P('expert', None, 'tensor'), may hold values from -0.1875 to 0.1875
Outputs:
- result: bfloat16 [2, 4, 64, 7168], P(None, 'pipe', 'expert', 'tensor')
Inputs may be any that keep to these rules, and one draw needn't show every extreme that they name: `expert_ids`: each token names 2 different experts. Among the 16 tokens of one direction held by one index of the expert axis at one section, at most 12 name any one expert, and in every draw some expert is named by exactly 12 of them.
All inputs are finite; a program needn't handle non-finite values.
Results may differ from a plain program's by a relative error of at most 0.0065.
Values may be sent and summed in bfloat16 or wider, within the bound.
A program may use at most 64 MiB of HBM per device.

v0:
```python
import functools

import jax
import jax.numpy as jnp
from jax import lax
from jax.experimental import pallas as pl
from jax.experimental.pallas import tpu as pltpu
from jax.sharding import PartitionSpec as P

norm_eps = 1e-06
route_scale = 2.5
MESH = pl.DeviceIdType.MESH


def pieces_of(width, most):
    for count in range(most, 0, -1):
        if width % (count * 128) == 0:
            return count
    return 1


def layer(
    sizes, slots, feat, cols,
    stream, ids_ref, gain_hbm, router_ref, up_hbm, down_hbm, out_ref,
    up, down, arrived, send, recv, rows32, inner, part, parts_in, active, squares, squares_in,
    small, small_in, ret, back, weights, gain_ref,
    load_sem, shift_send, shift_recv, disp_send, disp_recv, ten_send, ten_recv, ret_send, ret_recv,
):
    n_pipe, n_exp, n_ten = sizes
    pipe, expert, tensor = lax.axis_index("pipe"), lax.axis_index("expert"), lax.axis_index("tensor")
    tokens, width = arrived.shape
    half = tokens // 2
    hidden_units = up.shape[1]
    experts = router_ref.shape[0]
    step_f, step_c = width // feat, hidden_units // cols

    def section(by):
        return (lax.rem(pipe + by + n_pipe, n_pipe), expert, tensor)

    def member(by):
        return (pipe, lax.rem(expert + by + n_exp, n_exp), tensor)

    def holder(by):
        return (pipe, expert, lax.rem(tensor + by + n_ten, n_ten))

    barrier = pltpu.get_barrier_semaphore()
    greeted = [section(1), section(-1)]
    greeted += [member(o) for o in range(1, n_exp)] + [holder(o) for o in range(1, n_ten)]
    for who in greeted:
        pl.semaphore_signal(barrier, inc=1, device_id=who, device_id_type=MESH)

    loads = []
    for f in range(feat):
        at = pl.ds(f * step_f, step_f)
        loads.append(pltpu.make_async_copy(up_hbm.at[0, at], up.at[at], load_sem.at[f]))
    loads.append(pltpu.make_async_copy(down_hbm.at[0], down, load_sem.at[feat]))
    gain_load = pltpu.make_async_copy(
        gain_hbm, gain_ref.at[:, pl.ds(0, width)], load_sem.at[feat + 1]
    )
    gain_load.start()
    for load in loads:
        load.start()
    pl.semaphore_wait(barrier, len(greeted))

    shifts = [
        pltpu.make_async_remote_copy(
            src_ref=stream.at[d, 0], dst_ref=arrived.at[pl.ds(d * half, half)],
            send_sem=shift_send.at[d], recv_sem=shift_recv.at[d],
            device_id=section(1 - 2 * d), device_id_type=MESH,
        )
        for d in range(2)
    ]
    for copy in shifts:
        copy.start()

    ids = ids_ref[...]
    total = n_exp * slots
    lane = lax.broadcasted_iota(jnp.int32, (tokens, total), 1)
    block = lane // slots
    lane_expert = lax.rem(block + expert, n_exp)
    takes = jnp.zeros((tokens, total), jnp.float32)
    for k in range(ids.shape[1]):
        takes += jnp.where(ids[:, k : k + 1] == lane_expert, 1.0, 0.0)
    below = lax.broadcasted_iota(jnp.int32, (tokens, tokens), 0) > lax.broadcasted_iota(
        jnp.int32, (tokens, tokens), 1
    )
    rank = jnp.dot(
        jnp.where(below, 1.0, 0.0).astype(jnp.bfloat16),
        takes.astype(jnp.bfloat16),
        preferred_element_type=jnp.float32,
    )
    spot = (lane - block * slots).astype(jnp.float32)
    place = jnp.where((rank == spot) & (takes > 0.0), 1.0, 0.0)
    pick = place.astype(jnp.bfloat16)

    for copy in shifts:
        copy.wait_recv()

    dispatch = {}
    for f in range(feat):
        at = pl.ds(f * step_f, step_f)
        taken = lax.dot_general(
            pick, arrived[:, at], (((0,), (0,)), ((), ())), preferred_element_type=jnp.float32
        ).astype(jnp.float32)
        for o in list(range(1, n_exp)) + [0]:
            rows = taken[o * slots : (o + 1) * slots].astype(jnp.bfloat16)
            if o == 0:
                recv[0, 0:slots, at] = rows
                continue
            send[o, 0:slots, at] = rows
            dispatch[o, f] = pltpu.make_async_remote_copy(
                src_ref=send.at[o, pl.ds(0, slots), at], dst_ref=recv.at[o, pl.ds(0, slots), at],
                send_sem=disp_send.at[o, f], recv_sem=disp_recv.at[o, f],
                device_id=member(o), device_id_type=MESH,
            )
            dispatch[o, f].start()

    gain_load.wait()
    held = arrived[...].astype(jnp.float32)
    small[0] = jnp.broadcast_to(jnp.sum(held * held, axis=1, keepdims=True), (tokens, 128))
    small[1] = jnp.zeros((tokens, 128), jnp.float32)
    small[1, :, 0:experts] = lax.dot_general(
        held * gain_ref[:, 0:width], router_ref[...], (((1,), (1,)), ((), ())),
        preferred_element_type=jnp.float32, precision=lax.Precision.HIGHEST,
    )

    def to_holders(src, dst, sem):
        copies = [
            pltpu.make_async_remote_copy(
                src_ref=src, dst_ref=dst(o), send_sem=ten_send.at[o, sem], recv_sem=ten_recv.at[o, sem],
                device_id=holder(o), device_id_type=MESH,
            )
            for o in range(1, n_ten)
        ]
        for copy in copies:
            copy.start()
        return copies

    small_copies = to_holders(small, lambda o: small_in.at[o], cols)

    square = jnp.zeros((total, 1), jnp.float32)
    for f in range(feat):
        at = pl.ds(f * step_f, step_f)
        gain = gain_ref[:, at]
        for o in range(n_exp):
            if o > 0:
                dispatch[o, f].wait_recv()
            rows32[pl.ds(o * slots, slots), :] = recv[o, 0:slots, at].astype(jnp.float32)
        rows = rows32[...]
        square += jnp.sum(rows * rows, axis=1, keepdims=True)
        if f == feat - 1:
            squares[...] = jnp.broadcast_to(square, (total, 128))
            square_copies = to_holders(squares, lambda o: squares_in.at[o], cols + 1)
        lifted = (rows * gain).astype(jnp.bfloat16)
        loads[f].wait()
        if f < feat - 1:
            found = jnp.dot(lifted, up[at, :], preferred_element_type=jnp.float32)
            if f == 0:
                inner[...] = found
            else:
                inner[...] += found
    exchange = []
    for c in range(cols):
        units = pl.ds(c * step_c, step_c)
        found = jnp.dot(lifted, up[at, units], preferred_element_type=jnp.float32)
        if feat > 1:
            found += inner[:, units]
        inner[:, units] = found
        part[c] = found.astype(jnp.bfloat16)
        exchange.append(to_holders(part.at[c], lambda o, c=c: parts_in.at[o, c], c))

    for copy in small_copies:
        copy.wait_recv()
    sums, logits = small[0], small[1, :, 0:experts]
    for o in range(1, n_ten):
        sums = sums + small_in[o, 0]
        logits = logits + small_in[o, 1, :, 0:experts]
    full = float(width * n_ten)
    logits = logits * lax.rsqrt(sums[:, 0:1] / full + norm_eps)
    which = lax.broadcasted_iota(jnp.int32, logits.shape, 1)
    scores = []
    for k in range(ids.shape[1]):
        picked = jnp.sum(jnp.where(ids[:, k : k + 1] == which, logits, 0.0), axis=1, keepdims=True)
        scores.append(1.0 / (1.0 + jnp.exp(-picked)))
    norm = scores[0]
    for score in scores[1:]:
        norm = norm + score
    gate = jnp.zeros((tokens, total), jnp.float32)
    for k, score in enumerate(scores):
        gate += jnp.where(ids[:, k : k + 1] == lane_expert, route_scale * score / norm, 0.0)
    gate = gate * place
    coarse = gate.astype(jnp.bfloat16)
    weights[0, :, 0:total] = coarse
    weights[1, :, 0:total] = (gate - coarse.astype(jnp.float32)).astype(jnp.bfloat16)

    for copy in square_copies:
        copy.wait_recv()
    total_sq = squares[...]
    for o in range(1, n_ten):
        total_sq = total_sq + squares_in[o]
    inverse = lax.rsqrt(total_sq[:, 0:1] / full + norm_eps)
    for c in range(cols):
        units = pl.ds(c * step_c, step_c)
        for copy in exchange[c]:
            copy.wait_recv()
        value = inner[:, units]
        for o in range(1, n_ten):
            value = value + parts_in[o, c].astype(jnp.float32)
        value = value * inverse
        active[:, units] = (value / (1.0 + jnp.exp(-value))).astype(jnp.bfloat16)

    loads[feat].wait()
    returns = {}
    for f in range(feat):
        at = pl.ds(f * step_f, step_f)
        made = jnp.dot(active[...], down[:, at], preferred_element_type=jnp.float32)
        for o in list(range(1, n_exp)) + [0]:
            rows = made[o * slots : (o + 1) * slots].astype(jnp.bfloat16)
            if o == 0:
                back[0, 0:slots, at] = rows
                continue
            ret[o, 0:slots, at] = rows
            returns[o, f] = pltpu.make_async_remote_copy(
                src_ref=ret.at[o, pl.ds(0, slots), at], dst_ref=back.at[o, pl.ds(0, slots), at],
                send_sem=ret_send.at[o, f], recv_sem=ret_recv.at[o, f],
                device_id=member(-o), device_id_type=MESH,
            )
            returns[o, f].start()

    for f in range(feat):
        at = pl.ds(f * step_f, step_f)
        for o in range(n_exp):
            if o > 0:
                returns[o, f].wait_recv()
            rows32[pl.ds(o * slots, slots), :] = back[o, 0:slots, at].astype(jnp.float32)
        rows = rows32[...].astype(jnp.bfloat16)
        mixed = jnp.dot(weights[0, :, 0:total], rows, preferred_element_type=jnp.float32)
        mixed += jnp.dot(weights[1, :, 0:total], rows, preferred_element_type=jnp.float32)
        out_ref[:, at] = (arrived[:, at].astype(jnp.float32) + mixed).astype(jnp.bfloat16)

    for copies in [shifts, dispatch.values(), small_copies, square_copies, returns.values()] + exchange:
        for copy in copies:
            copy.wait_send()


def shards(sizes, stream, expert_ids, norm_gain, router, w_up, w_down):
    n_pipe, n_exp, n_ten = sizes
    tok_rows, width = stream.shape[2:]
    fanout = expert_ids.shape[-1]
    experts = router.shape[2]
    hidden_units = w_up.shape[2]
    tokens = 2 * tok_rows
    capacity = 3 * tok_rows * fanout // (2 * experts)
    slots = -(-2 * capacity // 8) * 8
    total = n_exp * slots
    feat = pieces_of(width, 4)
    cols = pieces_of(hidden_units, 4)
    bf16, f32 = jnp.bfloat16, jnp.float32
    dma = pltpu.SemaphoreType.DMA
    vmem = pl.BlockSpec(memory_space=pltpu.VMEM)
    hbm = pl.BlockSpec(memory_space=pl.ANY)
    result = pl.pallas_call(
        functools.partial(layer, sizes, slots, feat, cols),
        out_shape=jax.ShapeDtypeStruct((tokens, width), bf16),
        in_specs=[hbm, vmem, hbm, vmem, hbm, hbm],
        out_specs=vmem,
        scratch_shapes=[
            pltpu.VMEM((width, hidden_units), bf16),
            pltpu.VMEM((hidden_units, width), bf16),
            pltpu.VMEM((tokens, width), bf16),
            pltpu.VMEM((n_exp, -(-slots // 16) * 16, width), bf16),
            pltpu.VMEM((n_exp, -(-slots // 16) * 16, width), bf16),
            pltpu.VMEM((total, width // feat), f32),
            pltpu.VMEM((total, hidden_units), f32),
            pltpu.VMEM((cols, total, hidden_units // cols), bf16),
            pltpu.VMEM((n_ten, cols, total, hidden_units // cols), bf16),
            pltpu.VMEM((total, hidden_units), bf16),
            pltpu.VMEM((total, 128), f32),
            pltpu.VMEM((n_ten, total, 128), f32),
            pltpu.VMEM((2, tokens, 128), f32),
            pltpu.VMEM((n_ten, 2, tokens, 128), f32),
            pltpu.VMEM((n_exp, -(-slots // 16) * 16, width), bf16),
            pltpu.VMEM((n_exp, -(-slots // 16) * 16, width), bf16),
            pltpu.VMEM((2, tokens, -(-total // 128) * 128), bf16),
            pltpu.VMEM((1, width + 1024), f32),
            dma((feat + 2,)),
            dma((2,)),
            dma((2,)),
            dma((n_exp, feat)),
            dma((n_exp, feat)),
            dma((n_ten, cols + 2)),
            dma((n_ten, cols + 2)),
            dma((n_exp, feat)),
            dma((n_exp, feat)),
        ],
        compiler_params=pltpu.CompilerParams(
            collective_id=0, has_side_effects=True, vmem_limit_bytes=60 * 1024 * 1024
        ),
    )(stream, expert_ids.reshape(tokens, fanout), norm_gain, router[0].T, w_up, w_down)
    return result.reshape(2, 1, tok_rows, width)


def solution(mesh):
    sizes = tuple(mesh.shape[axis] for axis in ("pipe", "expert", "tensor"))
    return jax.shard_map(
        functools.partial(shards, sizes),
        mesh=mesh,
        in_specs=(
            P(None, "pipe", "expert", "tensor"),
            P(None, "pipe", "expert", None),
            P("pipe", "tensor"),
            P("pipe", "tensor", None),
            P("expert", "tensor", None),
            P("expert", None, "tensor"),
        ),
        out_specs=P(None, "pipe", "expert", "tensor"),
        check_vma=False,
    )
```

profile of v0, /device:TPU:0, one launch (start us, length us, event | category | flops | bytes accessed | tf_op | source)
XLA Modules:
  0.0 55.8 jit_solution(2057308630672818085)
XLA Ops:
  0.0 1.4 %copy.10 = s32[2,1,16,2]{3,2,0,1:T(8,128)} copy(s32[2,1,16,2]{2,3,1,0:T(2,128)} %param.7) | data formatting | bytes 512 | tf_op jit(solution)/shard_map/reshape | solution.py:299
  1.4 52.7 %shard_map.64 = bf16[32,3584]{1,0:T(8,128)(2,1)} custom-call(bf16[2,1,16,3584]{3,2,1,0:T(8,128)(2,1)} %stream.1, s32[32,2]{1,0:T(8,128)} %bitcast.8, f32[1,3584]{1,0:T(1,128)} %gain_hbm.1, f32[4,3584]{1,0:T(4,128)} %bitcast.9, bf16[1,3584,1024]{2,1,0:T(8,128)(2,1)} %up_hbm.1, bf16[1,1024,3584]{2,1,0:T(8,128)(2,1)} %down_hbm.1), custom_call_target="tpu_custom_call" | custom-call | tf_op jit(solution)/shard_map/pallas_call | solution.py:262
  54.1 1.6 %copy.13 = bf16[2,1,16,3584]{3,2,1,0:T(8,128)(2,1)} copy(bf16[2,1,16,3584]{3,2,1,0:T(8,128)(2,1)} %bitcast.7) | data formatting | bytes 458752
where the time goes:
time: 56 us; the launch traced here: 55.8 us
  Pallas kernels  52.7 us (94%)
  local copies, waits for them, and re-layouts  3.01 us (5%)
    pallas_call x1, Pallas kernels, shards(): pl.pallas_call(functools.partial(layer, sizes, slots, feat, cols), out_sh...  52.7 us
    unnamed x1, local copies, waits for them, and re-layouts  1.64 us
    reshape x1, local copies, waits for them, and re-layouts, shards(): expert_ids.reshape(tokens, fanout)  1.37 us

commit v1 on v0

--- a/solution.py
+++ b/solution.py
@@ -243,8 +243,421 @@
             copy.wait_send()
 
 
+def relay(
+    sizes, pieces,
+    stream, ids_ref, gain_hbm, router_hbm, up_hbm, down_hbm, out_hbm,
+    up, down, mine, arrived, pool, inner, part, part_in, small, small_in, meta, acc, opp_made,
+    ret_send, ret_in, comb_in, res, gain_ref, router_ref,
+    load_sem, out_sem, shift_send, shift_recv, disp_send, disp_recv, ten_send, ten_recv,
+    meta_send, meta_recv, rets_send, rets_recv, comb_recv,
+):
+    n_pipe, n_exp, n_ten = sizes
+    pipe, expert, tensor = lax.axis_index("pipe"), lax.axis_index("expert"), lax.axis_index("tensor")
+    rows, width = arrived.shape[1:]
+    hidden_units = up.shape[1]
+    experts = router_ref.shape[0]
+    step = width // pieces
+    bf16, f32 = jnp.bfloat16, jnp.float32
+
+    side = expert // 2
+    inside = lax.rem((expert + 1) // 2, 2)
+    outside = 1 - inside
+
+    def at_expert(z):
+        return (pipe, z, tensor)
+
+    partner = at_expert(expert + 1 - 2 * lax.rem(expert, 2))
+    across = [at_expert(2 - side), at_expert(3 - 3 * side)]
+    holder = (pipe, expert, 1 - tensor)
+    after, before = lax.rem(pipe + 1, n_pipe), lax.rem(pipe + n_pipe - 1, n_pipe)
+    sections = [(after, expert, tensor), (before, expert, tensor)]
+
+    barrier = pltpu.get_barrier_semaphore()
+    for who in sections + [holder, partner, across[0]]:
+        pl.semaphore_signal(barrier, inc=1, device_id=who, device_id_type=MESH)
+
+    @pl.when(inside == 1)
+    def _():
+        pl.semaphore_signal(barrier, inc=1, device_id=across[1], device_id_type=MESH)
+
+    spans = [pl.ds(f * step, step) for f in range(pieces)]
+    mine_load = pltpu.make_async_copy(stream.at[:, 0], mine, load_sem.at[0])
+    gain_load = pltpu.make_async_copy(gain_hbm, gain_ref.at[:, pl.ds(0, width)], load_sem.at[1])
+    router_load = pltpu.make_async_copy(router_hbm, router_ref, load_sem.at[2])
+    up_loads = [
+        pltpu.make_async_copy(up_hbm.at[0, at], up.at[at], load_sem.at[3 + f])
+        for f, at in enumerate(spans)
+    ]
+    down_load = pltpu.make_async_copy(down_hbm.at[0], down, load_sem.at[3 + pieces])
+    for load in [mine_load, gain_load, router_load] + up_loads + [down_load]:
+        load.start()
+
+    def heading(c):
+        return lax.rem(pipe + 1 + c, 2)
+
+    lane = lax.broadcasted_iota(jnp.int32, (rows, 128), 1)
+    square = (rows, rows)
+    eye = jnp.where(
+        lax.broadcasted_iota(jnp.int32, square, 0) == lax.broadcasted_iota(jnp.int32, square, 1), 1.0, 0.0
+    ).astype(bf16)
+    both = ids_ref[...]
+    kind = lax.broadcasted_iota(jnp.int32, (128, rows), 0)
+    named = []
+    for d in range(2):
+        marks = jnp.zeros((128, rows), f32)
+        for k in range(both.shape[1]):
+            marks += jnp.where(both[d, k : k + 1, :] == kind, 1.0, 0.0)
+        named.append(
+            lax.dot_general(eye, marks.astype(bf16), (((1,), (1,)), ((), ())), preferred_element_type=f32)
+        )
+    chosen = [jnp.where(heading(c) == 0, named[0], named[1]) for c in range(2)]
+
+    mine_load.wait()
+    pl.semaphore_wait(barrier, 5 + inside)
+
+    def remote(src, dst, send, recv, who):
+        return pltpu.make_async_remote_copy(
+            src_ref=src, dst_ref=dst, send_sem=send, recv_sem=recv, device_id=who, device_id_type=MESH
+        )
+
+    started, inner_only, outer_only = [], [], []
+    lands = [lax.rem(after + 1, 2), lax.rem(before, 2)]
+    shifts = [
+        remote(
+            mine.at[d], arrived.at[lands[d]], shift_send.at[d], shift_recv.at[lands[d]], sections[d]
+        )
+        for d in range(2)
+    ]
+    for copy in shifts:
+        copy.start()
+        started.append(copy)
+
+    own, mate = pl.ds(0, rows), pl.ds(rows, rows)
+    gain_load.wait()
+    router_load.wait()
+
+    def take_in(c):
+        remote(mine.at[0], arrived.at[c], shift_send.at[0], shift_recv.at[c], sections[0]).wait_recv()
+        for at in spans:
+            pool[c, 0, 0:rows, at] = (arrived[c, :, at].astype(f32) * gain_ref[:, at]).astype(bf16)
+        copies = [
+            remote(
+                pool.at[c, 0, own, at], pool.at[c, 0, mate, at],
+                disp_send.at[0, c, f], disp_recv.at[0, c, f], partner,
+            )
+            for f, at in enumerate(spans)
+        ]
+        there = pl.ds(pl.multiple_of(rows * outside, rows), rows)
+        copies += [
+            remote(
+                pool.at[c, 0, own, at], pool.at[c, 1, there, at],
+                disp_send.at[1, c, f], disp_recv.at[1 + outside, c, f], across[0],
+            )
+            for f, at in enumerate(spans)
+        ]
+        for copy in copies:
+            copy.start()
+            started.append(copy)
+        total = jnp.zeros((rows, 1), f32)
+        found = [jnp.zeros((rows, 1), f32) for _ in range(experts)]
+        for at in spans:
+            held = arrived[c, :, at].astype(f32)
+            total += jnp.sum(held * held, axis=1, keepdims=True)
+            lifted = held * gain_ref[:, at]
+            routes = router_ref[:, at]
+            for x in range(experts):
+                found[x] += jnp.sum(lifted * routes[x : x + 1], axis=1, keepdims=True)
+        tile = jnp.where(lane == experts, total, 0.0)
+        for x in range(experts):
+            tile = jnp.where(lane == x, found[x], tile)
+        small[c] = tile
+        copy = remote(
+            small.at[c], small_in.at[c], ten_send.at[6 + c], ten_recv.at[6 + c], holder
+        )
+        copy.start()
+        started.append(copy)
+        return copy
+
+    full = float(width * n_ten)
+
+    def weigh(c, copy):
+        copy.wait_recv()
+        tile = small[c] + small_in[c]
+        inverse = lax.rsqrt(tile[:, experts : experts + 1] / full + norm_eps)
+        scores = 1.0 / (1.0 + jnp.exp(-(tile * inverse)))
+        scores = jnp.where(chosen[c] > 0.0, scores, 0.0)
+        norm = jnp.sum(scores, axis=1, keepdims=True)
+        meta[c, 0, 0:rows] = jnp.where(lane == experts, inverse, route_scale * scores / norm)
+        there = pl.ds(pl.multiple_of(rows * outside, rows), rows)
+        copies = [
+            remote(meta.at[c, 0, own], meta.at[c, 0, mate], meta_send.at[0, c], meta_recv.at[0, c], partner),
+            remote(
+                meta.at[c, 0, own], meta.at[c, 1, there],
+                meta_send.at[1, c], meta_recv.at[1 + outside, c], across[0],
+            ),
+        ]
+        for copy in copies:
+            copy.start()
+            started.append(copy)
+
+    def forward(c, j):
+        spot = pl.ds(j * rows, rows)
+        copies = [
+            remote(
+                pool.at[c, 1, spot, at], pool.at[c, 1, spot, at],
+                disp_send.at[2 + j, c, f], disp_recv.at[1 + j, c, f], partner,
+            )
+            for f, at in enumerate(spans)
+        ]
+
+        @pl.when(inside == 1)
+        def _():
+            for copy in copies:
+                copy.wait_recv()
+                copy.start()
+
+        inner_only.extend(copies)
+
+    def forward_meta(c, j):
+        spot = pl.ds(j * rows, rows)
+        copy = remote(
+            meta.at[c, 1, spot], meta.at[c, 1, spot],
+            meta_send.at[2 + j, c], meta_recv.at[1 + j, c], partner,
+        )
+
+        @pl.when(inside == 1)
+        def _():
+            copy.wait_recv()
+            copy.start()
+
+        inner_only.append(copy)
+
+    passes = [(0, 0, 0, 2), (1, 0, 0, 2), (0, 1, 0, 1), (0, 1, 1, 1), (1, 1, 0, 1), (1, 1, 1, 1)]
+    loaded = set()
+    exchange = {}
+
+    def go_up(p):
+        c, g, first, many = passes[p]
+        spot = pl.ds(first * rows, many * rows)
+        total = None
+        for f, at in enumerate(spans):
+            if g == 0:
+                remote(
+                    pool.at[c, 0, own, at], pool.at[c, 0, mate, at],
+                    disp_send.at[0, c, f], disp_recv.at[0, c, f], partner,
+                ).wait_recv()
+            else:
+                waits = remote(
+                    pool.at[c, 1, spot, at], pool.at[c, 1, spot, at],
+                    disp_send.at[2 + first, c, f], disp_recv.at[1 + first, c, f], partner,
+                )
+                pl.when(outside == 1)(waits.wait_recv)
+            if f not in loaded:
+                up_loads[f].wait()
+                loaded.add(f)
+            found = jnp.dot(pool[c, g, spot, at], up[at, :], preferred_element_type=f32)
+            if f > 0:
+                found += inner[c, g, spot, :]
+            inner[c, g, spot, :] = found
+        part[c, g, spot, :] = found.astype(bf16)
+        exchange[p] = remote(
+            part.at[c, g, spot], part_in.at[c, g, spot], ten_send.at[p], ten_recv.at[p], holder
+        )
+        exchange[p].start()
+        started.append(exchange[p])
+
+    def go_down(p):
+        c, g, first, many = passes[p]
+        spot = pl.ds(first * rows, many * rows)
+        if g == 0:
+            remote(
+                meta.at[c, 0, own], meta.at[c, 0, mate], meta_send.at[0, c], meta_recv.at[0, c], partner
+            ).wait_recv()
+        else:
+            waits = remote(
+                meta.at[c, 1, spot], meta.at[c, 1, spot],
+                meta_send.at[2 + first, c], meta_recv.at[1 + first, c], partner,
+            )
+            pl.when(outside == 1)(waits.wait_recv)
+        tile = meta[c, g, spot]
+        wide = lax.broadcasted_iota(jnp.int32, tile.shape, 1)
+        gate = jnp.sum(jnp.where(wide == expert, tile, 0.0), axis=1, keepdims=True)
+        inverse = tile[:, experts : experts + 1]
+        exchange[p].wait_recv()
+        value = (inner[c, g, spot, :] + part_in[c, g, spot, :].astype(f32)) * inverse
+        active = (gate * (value / (1.0 + jnp.exp(-value)))).astype(bf16)
+        if p == 0:
+            down_load.wait()
+        for f, at in enumerate(spans):
+            made = jnp.dot(active, down[:, at], preferred_element_type=f32)
+            if g == 0:
+                acc[c, :, at] = arrived[c, :, at].astype(f32) + made[0:rows]
+                ret_send[c, 0, :, at] = made[rows:].astype(bf16)
+                copy = remote(
+                    ret_send.at[c, 0, :, at], ret_in.at[c, 0, :, at],
+                    rets_send.at[0, c, f], rets_recv.at[0, c, f], partner,
+                )
+                copy.start()
+                started.append(copy)
+                continue
+            copy = remote(
+                ret_send.at[c, 1 + first, :, at], comb_in.at[c, first, :, at],
+                rets_send.at[1 + first, c, f], comb_recv.at[first, c, f], partner,
+            )
+            outer_only.append(copy)
+
+            @pl.when(outside == 1)
+            def _():
+                ret_send[c, 1 + first, :, at] = made.astype(bf16)
+                copy.start()
+
+            @pl.when(inside == 1)
+            def _():
+                opp_made[c, first, :, at] = made
+
+    def combine(c, j):
+        for f, at in enumerate(spans):
+            waits = remote(
+                ret_send.at[c, 1 + j, :, at], comb_in.at[c, j, :, at],
+                rets_send.at[1 + j, c, f], comb_recv.at[j, c, f], partner,
+            )
+            copy = remote(
+                ret_send.at[c, 1 + j, :, at], ret_in.at[c, 1, :, at],
+                rets_send.at[1 + j, c, f], rets_recv.at[1, c, f], across[j],
+            )
+            inner_only.append(copy)
+
+            @pl.when(inside == 1)
+            def _():
+                waits.wait_recv()
+                ret_send[c, 1 + j, :, at] = (
+                    opp_made[c, j, :, at] + comb_in[c, j, :, at].astype(f32)
+                ).astype(bf16)
+                copy.start()
+
+    outs = []
+
+    def finish(c):
+        for f, at in enumerate(spans):
+            for k in range(2):
+                remote(
+                    ret_send.at[c, 0, :, at], ret_in.at[c, k, :, at],
+                    rets_send.at[0, c, f], rets_recv.at[k, c, f], partner,
+                ).wait_recv()
+            total = acc[c, :, at] + ret_in[c, 0, :, at].astype(f32) + ret_in[c, 1, :, at].astype(f32)
+            res[c, :, at] = total.astype(bf16)
+        copy = pltpu.make_async_copy(res.at[c], out_hbm.at[heading(c)], out_sem.at[c])
+        copy.start()
+        outs.append(copy)
+
+    near = take_in(0)
+    far = take_in(1)
+    weigh(0, near)
+    forward(0, 0)
+    go_up(0)
+    weigh(1, far)
+    forward(0, 1)
+    forward_meta(0, 0)
+    forward_meta(0, 1)
+    go_up(1)
+    forward(1, 0)
+    go_down(0)
+    go_up(2)
+    forward(1, 1)
+    forward_meta(1, 0)
+    forward_meta(1, 1)
+    go_down(1)
+    go_up(3)
+    go_down(2)
+    go_up(4)
+    go_down(3)
+    go_up(5)
+    go_down(4)
+    go_down(5)
+    combine(0, 0)
+    combine(0, 1)
+    finish(0)
+    combine(1, 0)
+    combine(1, 1)
+    finish(1)
+
+    for copy in started:
+        copy.wait_send()
+
+    @pl.when(inside == 1)
+    def _():
+        for copy in inner_only:
+            copy.wait_send()
+
+    @pl.when(outside == 1)
+    def _():
+        for copy in outer_only:
+            copy.wait_send()
+
+    for copy in outs:
+        copy.wait()
+
+
+def relayed(sizes, stream, expert_ids, norm_gain, router, w_up, w_down):
+    n_pipe, n_exp, n_ten = sizes
+    rows, width = stream.shape[2:]
+    experts = router.shape[2]
+    hidden_units = w_up.shape[2]
+    pieces = pieces_of(width, 4)
+    bf16, f32 = jnp.bfloat16, jnp.float32
+    dma = pltpu.SemaphoreType.DMA
+    vmem = pl.BlockSpec(memory_space=pltpu.VMEM)
+    hbm = pl.BlockSpec(memory_space=pl.ANY)
+    result = pl.pallas_call(
+        functools.partial(relay, sizes, pieces),
+        out_shape=jax.ShapeDtypeStruct((2, rows, width), bf16),
+        in_specs=[hbm, vmem, hbm, hbm, hbm, hbm],
+        out_specs=hbm,
+        scratch_shapes=[
+            pltpu.VMEM((width, hidden_units), bf16),
+            pltpu.VMEM((hidden_units, width), bf16),
+            pltpu.VMEM((2, rows, width), bf16),
+            pltpu.VMEM((2, rows, width), bf16),
+            pltpu.VMEM((2, 2, 2 * rows, width), bf16),
+            pltpu.VMEM((2, 2, 2 * rows, hidden_units), f32),
+            pltpu.VMEM((2, 2, 2 * rows, hidden_units), bf16),
+            pltpu.VMEM((2, 2, 2 * rows, hidden_units), bf16),
+            pltpu.VMEM((2, rows, 128), f32),
+            pltpu.VMEM((2, rows, 128), f32),
+            pltpu.VMEM((2, 2, 2 * rows, 128), f32),
+            pltpu.VMEM((2, rows, width), f32),
+            pltpu.VMEM((2, 2, rows, width), f32),
+            pltpu.VMEM((2, 3, rows, width), bf16),
+            pltpu.VMEM((2, 2, rows, width), bf16),
+            pltpu.VMEM((2, 2, rows, width), bf16),
+            pltpu.VMEM((2, rows, width), bf16),
+            pltpu.VMEM((1, width + 1024), f32),
+            pltpu.VMEM((experts, width), f32),
+            dma((4 + pieces,)),
+            dma((2,)),
+            dma((2,)),
+            dma((2,)),
+            dma((4, 2, pieces)),
+            dma((3, 2, pieces)),
+            dma((8,)),
+            dma((8,)),
+            dma((4, 2)),
+            dma((3, 2)),
+            dma((3, 2, pieces)),
+            dma((2, 2, pieces)),
+            dma((2, 2, pieces)),
+        ],
+        compiler_params=pltpu.CompilerParams(
+            collective_id=0, has_side_effects=True, vmem_limit_bytes=60 * 1024 * 1024
+        ),
+    )(stream, expert_ids[:, 0].transpose(0, 2, 1), norm_gain, router[0].T, w_up, w_down)
+    return result.reshape(2, 1, rows, width)
+
+
 def shards(sizes, stream, expert_ids, norm_gain, router, w_up, w_down):
     n_pipe, n_exp, n_ten = sizes
+    if n_exp == 4 and n_ten == 2 and n_pipe > 1 and n_pipe % 2 == 0 and router.shape[2] == n_exp:
+        return relayed(sizes, stream, expert_ids, norm_gain, router, w_up, w_down)
     tok_rows, width = stream.shape[2:]
     fanout = expert_ids.shape[-1]
     experts = router.shape[2]

time: 56 us -> 52.1 us (0.930)
  Pallas kernels: 52.7 us -> 50.3 us
  local copies, waits for them, and re-layouts: 3.01 us -> 1.64 us
    pallas_call x1, Pallas kernels: 52.7 us -> 50.3 us  [relayed(): pl.pallas_call(functools.partial(relay, sizes, pieces), out_shape=jax.Sha...]
    reshape x1 -> x0, local copies, waits for them, and re-layouts: 1.37 us -> none  [shards(): expert_ids.reshape(tokens, fanout)]
where the time goes in v1:
time: 52.1 us; the launch traced here: 51.9 us
  Pallas kernels  50.3 us (97%)
  local copies, waits for them, and re-layouts  1.64 us (3%)
    pallas_call x1, Pallas kernels, relayed(): pl.pallas_call(functools.partial(relay, sizes, pieces), out_shape=jax.Sha...  50.3 us
    unnamed x1, local copies, waits for them, and re-layouts  1.64 us

profile of v1, /device:TPU:0, one launch (start us, length us, event | category | flops | bytes accessed | tf_op | source)
XLA Modules:
  0.0 51.9 jit_solution(7403975123691748321)
XLA Ops:
  0.0 50.3 %shard_map.64 = bf16[2,16,3584]{2,1,0:T(8,128)(2,1)} custom-call(bf16[2,1,16,3584]{3,2,1,0:T(8,128)(2,1)} %stream.1, s32[2,2,16]{2,1,0:T(2,128)} %bitcast.11, f32[1,3584]{1,0:T(1,128)} %gain_hbm.1, f32[4,3584]{1,0:T(4,128)} %bitcast.10, bf16[1,3584,1024]{2,1,0:T(8,128)(2,1)} %up_hbm.1, bf16[1,1024,3584]{2,1,0:T(8,128)(2,1)} %down_hbm.1), custom_call_target="tpu_custom_call" | custom-call | tf_op jit(solution)/shard_map/pallas_call | solution.py:611
  50.3 1.6 %copy.9 = bf16[2,1,16,3584]{3,2,1,0:T(8,128)(2,1)} copy(bf16[2,1,16,3584]{3,2,1,0:T(8,128)(2,1)} %bitcast.9) | data formatting | bytes 458752

commit v2 on v0

--- a/solution.py
+++ b/solution.py
@@ -243,8 +243,499 @@
             copy.wait_send()
 
 
+def relay(
+    sizes, cap,
+    stream, ids_hbm, gain_hbm, router_hbm, up_hbm, down_hbm, out_ref,
+    ids_ref, up, down, mine, arrived, pool, inner, part, part_in, active, small, small_in, meta, acc, opp_made,
+    lhs, spare, pack_out, pack_in, ret_send, ret_in, gain_ref, router_ref,
+    load_sem, shift_send, shift_recv, disp_send, disp_recv, ten_send, ten_recv,
+    meta_send, meta_recv, rets_send, rets_recv, pack_send, pack_recv,
+):
+    n_pipe, n_exp, n_ten = sizes
+    pipe, expert, tensor = lax.axis_index("pipe"), lax.axis_index("expert"), lax.axis_index("tensor")
+    rows, width = arrived.shape[1:]
+    experts = router_ref.shape[0]
+    bf16, f32 = jnp.bfloat16, jnp.float32
+    half = width // 2
+    first_part = -(-half // 512) * 256
+    subs = [(0, first_part), (first_part, half - first_part)]
+    spans = [pl.ds(h * half + at, wide) for h in range(2) for at, wide in subs]
+    base = experts + 1
+    mate_id = expert + 1 - 2 * lax.rem(expert, 2)
+
+    side = expert // 2
+    inside = lax.rem((expert + 1) // 2, 2)
+    partner = (pipe, expert + 1 - 2 * lax.rem(expert, 2), tensor)
+    across, beyond = (pipe, 2 - side, tensor), (pipe, 3 - 3 * side, tensor)
+    holder = (pipe, expert, 1 - tensor)
+    after, before = lax.rem(pipe + 1, n_pipe), lax.rem(pipe + n_pipe - 1, n_pipe)
+    sections = [(after, expert, tensor), (before, expert, tensor)]
+
+    barrier = pltpu.get_barrier_semaphore()
+    for who in sections + [holder, partner]:
+        pl.semaphore_signal(barrier, inc=1, device_id=who, device_id_type=MESH)
+
+    @pl.when(inside == 1)
+    def _():
+        pl.semaphore_signal(barrier, inc=1, device_id=across, device_id_type=MESH)
+
+    mine_load = pltpu.make_async_copy(stream.at[:, 0], mine, load_sem.at[0])
+    gain_load = pltpu.make_async_copy(gain_hbm, gain_ref.at[:, pl.ds(0, width)], load_sem.at[1])
+    router_load = pltpu.make_async_copy(router_hbm, router_ref, load_sem.at[2])
+    down_load = pltpu.make_async_copy(down_hbm.at[0], down, load_sem.at[3])
+    ids_load = pltpu.make_async_copy(ids_hbm, ids_ref, load_sem.at[4])
+    up_loads = [
+        pltpu.make_async_copy(up_hbm.at[0, at], up.at[at], load_sem.at[5 + f])
+        for f, at in enumerate(spans)
+    ]
+    for load in [mine_load, ids_load, gain_load, router_load] + up_loads + [down_load]:
+        load.start()
+
+    def heading(c):
+        return lax.rem(pipe + 1 + c, 2)
+
+    mine_load.wait()
+    pl.semaphore_wait(barrier, 4 + inside)
+
+    def remote(src, dst, send, recv, who):
+        return pltpu.make_async_remote_copy(
+            src_ref=src, dst_ref=dst, send_sem=send, recv_sem=recv, device_id=who, device_id_type=MESH
+        )
+
+    lands = [lax.rem(after + 1, 2), lax.rem(before, 2)]
+    shifts = [
+        remote(
+            mine.at[d], arrived.at[lands[d]], shift_send.at[d], shift_recv.at[lands[d]], sections[d]
+        )
+        for d in range(2)
+    ]
+    for copy in shifts:
+        copy.start()
+
+    own, mate = pl.ds(0, rows), pl.ds(rows, rows)
+    full = float(width * n_ten)
+    gain_load.wait()
+    router_load.wait()
+
+    lane = lax.broadcasted_iota(jnp.int32, (rows, 128), 1)
+    square = (rows, rows)
+    eye = jnp.where(
+        lax.broadcasted_iota(jnp.int32, square, 0) == lax.broadcasted_iota(jnp.int32, square, 1), 1.0, 0.0
+    ).astype(bf16)
+    ids_load.wait()
+    both = ids_ref[...]
+    kind = lax.broadcasted_iota(jnp.int32, (128, rows), 0)
+    named = []
+    for d in range(2):
+        marks = jnp.zeros((128, rows), f32)
+        for k in range(both.shape[1]):
+            named_id = both[d, k : k + 1, :]
+            marks += jnp.where((named_id == kind) | (named_id + base == kind), 1.0, 0.0)
+        named.append(
+            lax.dot_general(eye, marks.astype(bf16), (((1,), (1,)), ((), ())), preferred_element_type=f32)
+        )
+    chosen = [jnp.where(heading(c) == 0, named[0], named[1]) for c in range(2)]
+    earlier = jnp.where(
+        lax.broadcasted_iota(jnp.int32, square, 0) > lax.broadcasted_iota(jnp.int32, square, 1), 1.0, 0.0
+    ).astype(bf16)
+    slots = [
+        jnp.where(mark > 0.0, jnp.dot(earlier, mark.astype(bf16), preferred_element_type=f32), -1.0)
+        for mark in chosen
+    ]
+    slot_id = lax.broadcasted_iota(jnp.int32, square, 1)
+
+    def picks(tile, who):
+        wide = lax.broadcasted_iota(jnp.int32, tile.shape, 1)
+        slot = jnp.sum(jnp.where(wide == base + who, tile, 0.0), axis=1, keepdims=True)
+        low = slot == slot_id.astype(f32)
+        high = slot == (slot_id - 4).astype(f32)
+        left = jnp.where(low & (slot_id < cap), 1.0, 0.0)
+        right = jnp.where((low & (slot_id < 8)) | (high & (slot_id >= 12)), 1.0, 0.0)
+        return left.astype(bf16), right.astype(bf16)
+
+    def perform(within):
+        started, loaded, exchange = list(shifts), set(), {}
+
+        def go(copy):
+            copy.start()
+            started.append(copy)
+
+        def rows_to(c, f, src, dst, send, recv, who):
+            return remote(
+                pool.at[c, *src, spans[f]], pool.at[c, *dst, spans[f]],
+                disp_send.at[send, c, f], disp_recv.at[recv, c, f], who,
+            )
+
+        def tile_to(c, src, dst, send, recv, who):
+            return remote(meta.at[c, *src], meta.at[c, *dst], meta_send.at[send, c], meta_recv.at[recv, c], who)
+
+        def spot(j):
+            return pl.ds(j * rows, rows)
+
+        def to_mate(c, f):
+            return rows_to(c, f, (0, own), (0, mate), 0, 0, partner)
+
+        def to_other(c, f, j):
+            return rows_to(c, f, (0, spot(j)), (1, spot(j)), 1 + j, 1 + j, across)
+
+        def relayed_rows(c, f, j):
+            return rows_to(c, f, (1, spot(j)), (1, spot(j)), 3 + j, 1 + j, partner)
+
+        def tile_mate(c):
+            return tile_to(c, (0, own), (0, mate), 0, 0, partner)
+
+        def tile_other(c, j):
+            return tile_to(c, (0, spot(j)), (1, spot(j)), 1 + j, 1 + j, across)
+
+        def relayed_tile(c, j):
+            return tile_to(c, (1, spot(j)), (1, spot(j)), 3 + j, 1 + j, partner)
+
+        def take_in(c):
+            remote(mine.at[0], arrived.at[c], shift_send.at[0], shift_recv.at[c], sections[0]).wait_recv()
+            for f, at in enumerate(spans):
+                pool[c, 0, 0:rows, at] = (arrived[c, :, at].astype(f32) * gain_ref[:, at]).astype(bf16)
+            for f in range(len(spans)):
+                go(to_mate(c, f))
+                if within and c == 0:
+                    go(to_other(c, f, 0))
+            total = jnp.zeros((rows, 1), f32)
+            found = [jnp.zeros((rows, 1), f32) for _ in range(experts)]
+            for at in spans:
+                held = arrived[c, :, at].astype(f32)
+                total += jnp.sum(held * held, axis=1, keepdims=True)
+                lifted = held * gain_ref[:, at]
+                routes = router_ref[:, at]
+                for x in range(experts):
+                    found[x] += jnp.sum(lifted * routes[x : x + 1], axis=1, keepdims=True)
+            tile = jnp.where(lane == experts, total, 0.0)
+            for x in range(experts):
+                tile = jnp.where(lane == x, found[x], tile)
+            small[c] = tile
+            copy = remote(small.at[c], small_in.at[c], ten_send.at[6 + c], ten_recv.at[6 + c], holder)
+            go(copy)
+            return copy
+
+        def weigh(c, copy):
+            copy.wait_recv()
+            tile = small[c] + small_in[c]
+            inverse = lax.rsqrt(tile[:, experts : experts + 1] / full + norm_eps)
+            scores = 1.0 / (1.0 + jnp.exp(-(tile * inverse)))
+            scores = jnp.where((chosen[c] > 0.0) & (lane < experts), scores, 0.0)
+            norm = jnp.sum(scores, axis=1, keepdims=True)
+            tile = jnp.where(lane == experts, inverse, route_scale * scores / norm)
+            meta[c, 0, 0:rows] = jnp.where(lane < base, tile, slots[c])
+            go(tile_mate(c))
+            if within:
+                go(tile_other(c, 0))
+
+        def send_across(c):
+            for f in range(len(spans)):
+                go(to_other(c, f, 0))
+
+        def relay_mate(c):
+            for f in range(len(spans)):
+                to_mate(c, f).wait_recv()
+                go(to_other(c, f, 1))
+
+        def relay_mate_tile(c):
+            tile_mate(c).wait_recv()
+            go(tile_other(c, 1))
+
+        def relay_rows(c, j):
+            for f in range(len(spans)):
+                copy = relayed_rows(c, f, j)
+                copy.wait_recv()
+                go(copy)
+
+        def relay_tile(c, j):
+            copy = relayed_tile(c, j)
+            copy.wait_recv()
+            go(copy)
+
+        def go_up(p, ready=None):
+            c, g, first, many = passes[p]
+            band = pl.ds(first * rows, many * rows)
+            if "up" not in loaded:
+                for load in up_loads:
+                    load.wait()
+                loaded.add("up")
+            if ready is not None:
+                heard(ready)
+            if within:
+                found = jnp.dot(pool[c, g, band, :], up[...], preferred_element_type=f32)
+            else:
+                bounds = [0, width - half, width] if g == 0 else [0, width]
+                for low, high in zip(bounds, bounds[1:]):
+                    for f in range(2 * low // half, 2 * high // half):
+                        (to_mate(c, f) if g == 0 else relayed_rows(c, f, first)).wait_recv()
+                    more = jnp.dot(
+                        pool[c, g, band, low:high], up[low:high, :], preferred_element_type=f32
+                    )
+                    found = more if low == 0 else found + more
+            if ready is not None:
+                activate(ready)
+            inner[c, g, band, :] = found
+            part[c, g, band, :] = found.astype(bf16)
+            exchange[p] = remote(
+                part.at[c, g, band], part_in.at[c, g, band], ten_send.at[p], ten_recv.at[p], holder
+            )
+            go(exchange[p])
+
+        def heard(p):
+            c, g, first, many = passes[p]
+            if not within:
+                (tile_mate(c) if g == 0 else relayed_tile(c, first)).wait_recv()
+            exchange[p].wait_recv()
+            loaded.add(p)
+
+        def activate(p):
+            c, g, first, many = passes[p]
+            band = pl.ds(first * rows, many * rows)
+            tile = meta[c, g, band]
+            wide = lax.broadcasted_iota(jnp.int32, tile.shape, 1)
+            gate = jnp.sum(jnp.where(wide == expert, tile, 0.0), axis=1, keepdims=True)
+            inverse = tile[:, experts : experts + 1]
+            value = (inner[c, g, band, :] + part_in[c, g, band, :].astype(f32)) * inverse
+            value = (gate * (value / (1.0 + jnp.exp(-value)))).astype(bf16)
+            if within:
+                active[c, g, band, :] = value
+                return
+            k = 0 if g == 0 else 1 + first
+            for h, pick in enumerate(picks(tile[-rows:], expert)):
+                if g == 0:
+                    lhs[c, k, h, rows : 2 * rows, :] = value[0:rows]
+                lhs[c, k, h, 0:rows, :] = lax.dot_general(
+                    pick, value[-rows:], (((0,), (0,)), ((), ())), preferred_element_type=f32
+                ).astype(bf16)
+
+        def packed(c, k, b):
+            return remote(
+                pack_out.at[c, k, b], pack_in.at[c, k, b], pack_send.at[k, c, b], pack_recv.at[k, c, b], partner
+            )
+
+        def go_down(p):
+            c, g, first, many = passes[p]
+            band = pl.ds(first * rows, many * rows)
+            if p not in loaded:
+                heard(p)
+                activate(p)
+            if "down" not in loaded:
+                down_load.wait()
+                loaded.add("down")
+            k = 0 if g == 0 else 1 + first
+
+            def deliver(f, made):
+                at = spans[f]
+                h, (low, wide) = f // 2, subs[f % 2]
+                if within and g == 0:
+                    acc[c, :, at] = arrived[c, :, at].astype(f32) + made[0:rows]
+                    ret_send[c, 0, :, at] = made[rows:].astype(bf16)
+                    go(back_to_mate(c, f))
+                elif within:
+                    for j in range(2):
+                        opp_made[c, j, :, at] = made[j * rows : (j + 1) * rows]
+                else:
+                    if g == 0:
+                        acc[c, :, at] = arrived[c, :, at].astype(f32) + made[rows:]
+                    local = pl.ds(low, wide)
+                    pack_out[c, k, h, :, local] = made[0:8].astype(bf16)
+                    if h == 0:
+                        spare[c, k, :, local] = made[8:16]
+                    else:
+                        pack_out[c, k, 2, :, local] = (spare[c, k, :, local] + made[8:16]).astype(bf16)
+                    if f == 1:
+                        go(packed(c, k, 0))
+                    if f == 3:
+                        go(packed(c, k, 2))
+                        go(packed(c, k, 1))
+
+            last = None
+            for f, at in enumerate(spans):
+                left = active[c, g, band, :] if within else lhs[c, k, f // 2, 0 : many * rows, :]
+                made = jnp.dot(left, down[:, at], preferred_element_type=f32)
+                if last is not None:
+                    deliver(f - 1, last)
+                last = made
+            deliver(len(spans) - 1, last)
+
+        def spread(c, k, f, pick):
+            h, (low, wide) = f // 2, subs[f % 2]
+            local = pl.ds(low, wide)
+            if f == 0:
+                packed(c, k, 0).wait_recv()
+                packed(c, k, 2).wait_recv()
+            if f == 2:
+                packed(c, k, 1).wait_recv()
+            got = jnp.concatenate(
+                [pack_in[c, k, h, :, local].astype(f32), pack_in[c, k, 2, :, local].astype(f32)], axis=0
+            ).astype(bf16)
+            return jnp.dot(pick[h], got, preferred_element_type=f32)
+
+        def absorb(c):
+            pick = picks(meta[c, 0, 0:rows], mate_id)
+            for f, at in enumerate(spans):
+                acc[c, :, at] += spread(c, 0, f, pick)
+
+        def back_to_mate(c, f):
+            at = spans[f]
+            return remote(
+                ret_send.at[c, 0, :, at], ret_in.at[c, 0, :, at],
+                rets_send.at[0, c, f], rets_recv.at[0, c, f], partner,
+            )
+
+        def sum_home(c, f, j):
+            at = spans[f]
+            return remote(
+                ret_send.at[c, 1 + j, :, at], ret_in.at[c, 1, :, at],
+                rets_send.at[1 + j, c, f], rets_recv.at[1, c, f], beyond if j else across,
+            )
+
+        def combine(c, j):
+            pick = picks(meta[c, 1, spot(j)], mate_id)
+            for f, at in enumerate(spans):
+                ret_send[c, 1 + j, :, at] = (
+                    opp_made[c, j, :, at] + spread(c, 1 + j, f, pick)
+                ).astype(bf16)
+                go(sum_home(c, f, j))
+
+        def finish(c):
+            for f, at in enumerate(spans):
+                total = acc[c, :, at]
+                if not within:
+                    back_to_mate(c, f).wait_recv()
+                    total += ret_in[c, 0, :, at].astype(f32)
+                sum_home(c, f, 0).wait_recv()
+                total += ret_in[c, 1, :, at].astype(f32)
+                out_ref[heading(c), :, at] = total.astype(bf16)
+
+        near = take_in(0)
+        far = take_in(1)
+        if within:
+            passes = [(0, 0, 0, 2), (0, 1, 0, 2), (1, 0, 0, 2), (1, 1, 0, 2)]
+            weigh(0, near)
+            relay_rows(0, 0)
+            relay_mate(0)
+            relay_mate(1)
+            relay_mate_tile(0)
+            send_across(1)
+            weigh(1, far)
+            go_up(0)
+            relay_rows(0, 1)
+            relay_tile(0, 0)
+            relay_mate_tile(1)
+            go_up(2)
+            relay_rows(1, 1)
+            relay_tile(0, 1)
+            go_up(1, 0)
+            relay_tile(1, 1)
+            relay_rows(1, 0)
+            go_up(3)
+            go_down(0)
+            relay_tile(1, 0)
+            go_down(2)
+            go_down(1)
+            go_down(3)
+            absorb(0)
+            absorb(1)
+            combine(0, 0)
+            combine(0, 1)
+            combine(1, 1)
+            combine(1, 0)
+        else:
+            passes = [(0, 0, 0, 2), (1, 0, 0, 2), (0, 1, 0, 1), (0, 1, 1, 1), (1, 1, 1, 1), (1, 1, 0, 1)]
+            weigh(0, near)
+            go_up(0)
+            weigh(1, far)
+            go_up(1)
+            go_down(0)
+            go_up(2)
+            go_down(1)
+            go_up(3)
+            go_up(4, 2)
+            go_down(2)
+            go_down(3)
+            go_up(5)
+            go_down(4)
+            go_down(5)
+        finish(0)
+        finish(1)
+        for copy in started:
+            copy.wait_send()
+
+    @pl.when(inside == 1)
+    def _():
+        perform(True)
+
+    @pl.when(inside == 0)
+    def _():
+        perform(False)
+
+
+def relayed(sizes, stream, expert_ids, norm_gain, router, w_up, w_down):
+    n_pipe, n_exp, n_ten = sizes
+    rows, width = stream.shape[2:]
+    experts, fanout = router.shape[2], expert_ids.shape[3]
+    hidden_units = w_up.shape[2]
+    cap = 3 * rows * fanout // (2 * experts)
+    pieces = 4
+    bf16, f32 = jnp.bfloat16, jnp.float32
+    dma = pltpu.SemaphoreType.DMA
+    vmem = pl.BlockSpec(memory_space=pltpu.VMEM)
+    hbm = pl.BlockSpec(memory_space=pl.ANY)
+    result = pl.pallas_call(
+        functools.partial(relay, sizes, cap),
+        out_shape=pltpu.VMEM((2, rows, width), bf16),
+        in_specs=[hbm] * 6,
+        out_specs=vmem,
+        scratch_shapes=[
+            pltpu.VMEM((2, fanout, rows), jnp.int32),
+            pltpu.VMEM((width, hidden_units), bf16),
+            pltpu.VMEM((hidden_units, width), bf16),
+            pltpu.VMEM((2, rows, width), bf16),
+            pltpu.VMEM((2, rows, width), bf16),
+            pltpu.VMEM((2, 2, 2 * rows, width), bf16),
+            pltpu.VMEM((2, 2, 2 * rows, hidden_units), f32),
+            pltpu.VMEM((2, 2, 2 * rows, hidden_units), bf16),
+            pltpu.VMEM((2, 2, 2 * rows, hidden_units), bf16),
+            pltpu.VMEM((2, 2, 2 * rows, hidden_units), bf16),
+            pltpu.VMEM((2, rows, 128), f32),
+            pltpu.VMEM((2, rows, 128), f32),
+            pltpu.VMEM((2, 2, 2 * rows, 128), f32),
+            pltpu.VMEM((2, rows, width), f32),
+            pltpu.VMEM((2, 2, rows, width), f32),
+            pltpu.VMEM((2, 3, 2, 2 * rows, hidden_units), bf16),
+            pltpu.VMEM((2, 3, 8, width // 2), f32),
+            pltpu.VMEM((2, 3, 3, 8, width // 2), bf16),
+            pltpu.VMEM((2, 3, 3, 8, width // 2), bf16),
+            pltpu.VMEM((2, 3, rows, width), bf16),
+            pltpu.VMEM((2, 2, rows, width), bf16),
+            pltpu.VMEM((1, width + 1024), f32),
+            pltpu.VMEM((experts, width), f32),
+            dma((5 + pieces,)),
+            dma((2,)),
+            dma((2,)),
+            dma((5, 2, pieces)),
+            dma((3, 2, pieces)),
+            dma((8,)),
+            dma((8,)),
+            dma((5, 2)),
+            dma((3, 2)),
+            dma((3, 2, pieces)),
+            dma((2, 2, pieces)),
+            dma((3, 2, 3)),
+            dma((3, 2, 3)),
+        ],
+        compiler_params=pltpu.CompilerParams(
+            collective_id=0, has_side_effects=True, vmem_limit_bytes=67043328 - 4 * rows * width - 16384
+        ),
+    )(stream, expert_ids[:, 0].transpose(0, 2, 1), norm_gain, router[0].T, w_up, w_down)
+    return result.reshape(2, 1, rows, width)
+
+
 def shards(sizes, stream, expert_ids, norm_gain, router, w_up, w_down):
     n_pipe, n_exp, n_ten = sizes
+    if n_exp == 4 and n_ten == 2 and n_pipe > 1 and n_pipe % 2 == 0 and router.shape[2] == n_exp:
+        return relayed(sizes, stream, expert_ids, norm_gain, router, w_up, w_down)
     tok_rows, width = stream.shape[2:]
     fanout = expert_ids.shape[-1]
     experts = router.shape[2]

time: 56 us -> 40.3 us (0.72)
  Pallas kernels: 52.7 us -> 39.5 us
  local copies, waits for them, and re-layouts: 3.01 us -> 0.69 us
    pallas_call x1, Pallas kernels: 52.7 us -> 39.5 us  [relayed(): pl.pallas_call(functools.partial(relay, sizes, cap), out_shape=pltpu.VMEM...]
    reshape x1 -> x0, local copies, waits for them, and re-layouts: 1.37 us -> none  [shards(): expert_ids.reshape(tokens, fanout)]
    unnamed x1, local copies, waits for them, and re-layouts: 1.64 us -> 0.69 us
where the time goes in v2:
time: 40.3 us; the launch traced here: 40.2 us
  Pallas kernels  39.5 us (98%)
  local copies, waits for them, and re-layouts  0.69 us (2%)
    pallas_call x1, Pallas kernels, relayed(): pl.pallas_call(functools.partial(relay, sizes, cap), out_shape=pltpu.VMEM...  39.5 us

profile of v2, /device:TPU:0, one launch (start us, length us, event | category | flops | bytes accessed | tf_op | source)
XLA Modules:
  0.0 40.2 jit_solution(16938907661937567099)
XLA Ops:
  0.0 39.5 %shard_map.64 = bf16[2,16,3584]{2,1,0:T(8,128)(2,1)S(1)} custom-call(bf16[2,1,16,3584]{3,2,1,0:T(8,128)(2,1)} %stream.1, s32[2,2,16]{2,1,0:T(2,128)} %bitcast.11, f32[1,3584]{1,0:T(1,128)} %gain_hbm.1, f32[4,3584]{1,0:T(4,128)} %bitcast.10, bf16[1,3584,1024]{2,1,0:T(8,128)(2,1)} %up_hbm.1, bf16[1,1024,3584]{2,1,0:T(8,128)(2,1)} %down_hbm.1), custom_call_target="tpu_custom_call" | custom-call | tf_op jit(solution)/shard_map/pallas_call | solution.py:685
  39.5 0.7 %copy.9 = bf16[2,1,16,3584]{3,2,1,0:T(8,128)(2,1)} copy(bf16[2,1,16,3584]{3,2,1,0:T(8,128)(2,1)S(1)} %bitcast.9) | data formatting | bytes 458752

commit v3 on v2

--- a/solution.py
+++ b/solution.py
@@ -398,6 +398,8 @@
                 go(to_mate(c, f))
                 if within and c == 0:
                     go(to_other(c, f, 0))
+            if within and c == 1:
+                send_across(1, 0, 2)
             total = jnp.zeros((rows, 1), f32)
             found = [jnp.zeros((rows, 1), f32) for _ in range(experts)]
             for at in spans:
@@ -428,8 +430,8 @@
             if within:
                 go(tile_other(c, 0))
 
-        def send_across(c):
-            for f in range(len(spans)):
+        def send_across(c, first, end):
+            for f in range(first, end):
                 go(to_other(c, f, 0))
 
         def relay_mate(c):
@@ -617,27 +619,27 @@
             relay_mate(0)
             relay_mate(1)
             relay_mate_tile(0)
-            send_across(1)
+            send_across(1, 2, 4)
             weigh(1, far)
             go_up(0)
             relay_rows(0, 1)
             relay_tile(0, 0)
             relay_mate_tile(1)
-            go_up(2)
+            go_up(1)
             relay_rows(1, 1)
             relay_tile(0, 1)
-            go_up(1, 0)
+            go_up(2)
             relay_tile(1, 1)
             relay_rows(1, 0)
             go_up(3)
+            relay_tile(1, 0)
+            go_down(1)
             go_down(0)
-            relay_tile(1, 0)
             go_down(2)
-            go_down(1)
-            go_down(3)
             absorb(0)
             absorb(1)
             combine(0, 0)
+            go_down(3)
             combine(0, 1)
             combine(1, 1)
             combine(1, 0)
@@ -647,12 +649,12 @@
             go_up(0)
             weigh(1, far)
             go_up(1)
+            go_up(2)
             go_down(0)
-            go_up(2)
             go_down(1)
             go_up(3)
-            go_up(4, 2)
             go_down(2)
+            go_up(4)
             go_down(3)
             go_up(5)
             go_down(4)

time: 40.3 us -> 38.6 us (0.958)
  Pallas kernels: 39.5 us -> 37.7 us
    pallas_call x1, Pallas kernels: 39.5 us -> 37.7 us  [relayed(): pl.pallas_call(functools.partial(relay, sizes, cap), out_shape=pltpu.VMEM...]
where the time goes in v3:
time: 38.6 us; the launch traced here: 38.4 us
  Pallas kernels  37.7 us (98%)
  local copies, waits for them, and re-layouts  0.69 us (2%)
    pallas_call x1, Pallas kernels, relayed(): pl.pallas_call(functools.partial(relay, sizes, cap), out_shape=pltpu.VMEM...  37.7 us

profile of v3, /device:TPU:0, one launch (start us, length us, event | category | flops | bytes accessed | tf_op | source)
XLA Modules:
  0.0 38.4 jit_solution(17085935719415679488)
XLA Ops:
  0.0 37.7 %shard_map.64 = bf16[2,16,3584]{2,1,0:T(8,128)(2,1)S(1)} custom-call(bf16[2,1,16,3584]{3,2,1,0:T(8,128)(2,1)} %stream.1, s32[2,2,16]{2,1,0:T(2,128)} %bitcast.11, f32[1,3584]{1,0:T(1,128)} %gain_hbm.1, f32[4,3584]{1,0:T(4,128)} %bitcast.10, bf16[1,3584,1024]{2,1,0:T(8,128)(2,1)} %up_hbm.1, bf16[1,1024,3584]{2,1,0:T(8,128)(2,1)} %down_hbm.1), custom_call_target="tpu_custom_call" | custom-call | tf_op jit(solution)/shard_map/pallas_call | solution.py:687
  37.7 0.7 %copy.9 = bf16[2,1,16,3584]{3,2,1,0:T(8,128)(2,1)} copy(bf16[2,1,16,3584]{3,2,1,0:T(8,128)(2,1)S(1)} %bitcast.9) | data formatting | bytes 458752

commit v4 on v3

--- a/solution.py
+++ b/solution.py
@@ -636,13 +636,13 @@
             go_down(1)
             go_down(0)
             go_down(2)
-            absorb(0)
-            absorb(1)
             combine(0, 0)
             go_down(3)
             combine(0, 1)
             combine(1, 1)
             combine(1, 0)
+            absorb(0)
+            absorb(1)
         else:
             passes = [(0, 0, 0, 2), (1, 0, 0, 2), (0, 1, 0, 1), (0, 1, 1, 1), (1, 1, 1, 1), (1, 1, 0, 1)]
             weigh(0, near)

time: 38.6 us -> 38.6 us (level)
  no operation moved by 1% of the time
where the time goes in v4:
time: 38.6 us; the launch traced here: 38.4 us
  Pallas kernels  37.7 us (98%)
  local copies, waits for them, and re-layouts  0.69 us (2%)
    pallas_call x1, Pallas kernels, relayed(): pl.pallas_call(functools.partial(relay, sizes, cap), out_shape=pltpu.VMEM...  37.7 us

profile of v4, /device:TPU:0, one launch (start us, length us, event | category | flops | bytes accessed | tf_op | source)
XLA Modules:
  0.0 38.4 jit_solution(1136412189488150608)
XLA Ops:
  0.0 37.7 %shard_map.64 = bf16[2,16,3584]{2,1,0:T(8,128)(2,1)S(1)} custom-call(bf16[2,1,16,3584]{3,2,1,0:T(8,128)(2,1)} %stream.1, s32[2,2,16]{2,1,0:T(2,128)} %bitcast.11, f32[1,3584]{1,0:T(1,128)} %gain_hbm.1, f32[4,3584]{1,0:T(4,128)} %bitcast.10, bf16[1,3584,1024]{2,1,0:T(8,128)(2,1)} %up_hbm.1, bf16[1,1024,3584]{2,1,0:T(8,128)(2,1)} %down_hbm.1), custom_call_target="tpu_custom_call" | custom-call | tf_op jit(solution)/shard_map/pallas_call | solution.py:687
  37.7 0.7 %copy.9 = bf16[2,1,16,3584]{3,2,1,0:T(8,128)(2,1)} copy(bf16[2,1,16,3584]{3,2,1,0:T(8,128)(2,1)S(1)} %bitcast.9) | data formatting | bytes 458752
